TPU v7x, 32 devices: a whole 2x2x4 slice. The times are simulated.
32 devices in a mesh: gx: 4 (over z), gy: 2 (over y), gz: 4 (over x, core).
Axes of the slice: x: 2, y: 2, z: 4, core: 2. Of those that a mesh axis runs over, the one named last changes fastest.
Arguments:
- atom_x: float32 [4, 8, 256], P('gx', ('gy', 'gz')), may hold values from 0 to 95.99
- atom_y: float32 [4, 8, 256], P('gx', ('gy', 'gz')), may hold values from 0 to 47.99
- atom_z: float32 [4, 8, 256], P('gx', ('gy', 'gz')), may hold values from 0 to 384
- charges: float32 [4, 8, 256], P('gx', ('gy', 'gz')), may hold values from -4.5 to 4.5
- counts: int32 [4, 8], P('gx', ('gy', 'gz')), may hold values from 32 to 256, as said below
- background: float32 [384, 384, 384], P(('gy', 'gz'), 'gx'), may hold values from -0.3125 to 0.3125
Outputs:
- forces: float32 [3, 4, 8, 256], P(None, 'gx', ('gy', 'gz'))
Inputs may be any that keep to these rules, and one draw needn't show every extreme that they name: `counts`: live slots come first in each pencil; some pencil is full in every draw.
All inputs are finite; a program needn't handle non-finite values.
Results may differ from a plain program's by a relative error of at most 0.0003.
Values sent between devices are 32-bit elements; how exact they have to be, the bound alone decides.
No kernel may reach another device: no remote copies, remote signals or barrier semaphores. Data moves between devices by JAX's collectives and lax.ppermute only.
A program may use at most 128 MiB of HBM per device.

v0:
```python
import math
import jax
import jax.numpy as jnp
from jax import lax
from jax.sharding import PartitionSpec as P

COULOMB = 6.5
EWALD_BETA = 1.0
PRECISE = lax.Precision.HIGHEST


def extended(block, sides, width):
    for axis, dim in sides:
        count = lax.axis_size(axis)
        forward = [(i, i + 1) for i in range(count - 1)]
        forward.append((count - 1, 0))
        backward = [(target, source) for source, target in forward]
        low = lax.ppermute(
            lax.slice_in_dim(block, block.shape[dim] - width, None, axis=dim), axis, forward
        )
        high = lax.ppermute(lax.slice_in_dim(block, 0, width, axis=dim), axis, backward)
        block = jnp.concatenate([low, block, high], axis=dim)
    return block


def spline(offset):
    distance = jnp.minimum(offset, 5.0 - offset)
    ramp_zero = jax.nn.relu(distance)
    ramp_one = jax.nn.relu(distance - 1.0)
    ramp_two = jax.nn.relu(distance - 2.0)
    cube_zero = ramp_zero * ramp_zero * ramp_zero
    cube_one = ramp_one * ramp_one * ramp_one
    cube_two = ramp_two * ramp_two * ramp_two
    height = (cube_zero * ramp_zero - 5.0 * cube_one * ramp_one + 10.0 * cube_two * ramp_two) / 24.0
    gradient = (cube_zero - 5.0 * cube_one + 10.0 * cube_two) / 6.0
    return (height, jnp.where(offset < 2.5, gradient, -gradient))


def weights(coord_x, coord_y, coord_z, cells_x, cells_y, depth):
    edge_x = jnp.arange(cells_x + 4).astype(jnp.float32)
    weight_x, slope_x = spline(coord_x[None, :] - edge_x[:, None] + 4.5)
    edge_y = jnp.arange(cells_y + 4).astype(jnp.float32)
    weight_y, slope_y = spline(coord_y[None, :] - edge_y[:, None] + 4.5)
    planes = jnp.arange(depth).astype(jnp.float32)
    halfway = depth / 2.0
    offset_z = jnp.mod(coord_z[:, None] - planes[None, :] + halfway, float(depth)) - halfway + 2.5
    weight_z, slope_z = spline(offset_z)
    return (weight_x, slope_x, weight_y, slope_y, weight_z, slope_z)


def deposit(stencil, charge_live):
    weight_x, slope_x, weight_y, slope_y, weight_z, slope_z = stencil
    mixed = weight_y[:, None, :] * weight_x[None, :, :] * charge_live[None, None, :]
    flat = mixed.reshape(-1, charge_live.shape[0])
    spread = jnp.dot(flat, weight_z, precision=PRECISE, preferred_element_type=jnp.float32)
    return spread.reshape(weight_y.shape[0], weight_x.shape[0], weight_z.shape[1])


def pull(potential, stencil, charge_live):
    weight_x, slope_x, weight_y, slope_y, weight_z, slope_z = stencil
    extent_y, extent_x, depth = potential.shape
    flat = potential.reshape(extent_y * extent_x, depth)
    dims = (((1,), (1,)), ((), ()))
    plain = lax.dot_general(
        flat, weight_z, dims, precision=PRECISE, preferred_element_type=jnp.float32
    )
    deriv = lax.dot_general(
        flat, slope_z, dims, precision=PRECISE, preferred_element_type=jnp.float32
    )
    plain = plain.reshape(extent_y, extent_x, -1)
    deriv = deriv.reshape(extent_y, extent_x, -1)
    along_x = jnp.sum(weight_x[None] * plain, axis=1)
    turned_x = jnp.sum(slope_x[None] * plain, axis=1)
    depth_x = jnp.sum(weight_x[None] * deriv, axis=1)
    force_x = -charge_live * jnp.sum(weight_y * turned_x, axis=0)
    force_y = -charge_live * jnp.sum(slope_y * along_x, axis=0)
    force_z = -charge_live * jnp.sum(weight_y * depth_x, axis=0)
    return jnp.stack([force_x, force_y, force_z])


def modulus(indices, length):
    angles = 2.0 * math.pi / length * indices.astype(jnp.float32)
    return (230.0 + 152.0 * jnp.cos(angles) + 2.0 * jnp.cos(2.0 * angles)) / 384.0


def frequency(indices, length):
    signed = jnp.where(indices <= length // 2, indices, indices - length)
    return signed.astype(jnp.float32) / length


def influence(wave_z, wave_x, wave_y, depth, width_x, width_y):
    freq_z = frequency(wave_z, depth)
    freq_x = frequency(wave_x, width_x)
    freq_y = frequency(wave_y, width_y)
    square = freq_z[:, None, None] ** 2 + freq_x[None, :, None] ** 2 + freq_y[None, None, :] ** 2
    damping = (
        modulus(wave_z, depth)[:, None, None]
        * modulus(wave_x, width_x)[None, :, None]
        * modulus(wave_y, width_y)[None, None, :]
    )
    bounded = jnp.where(square > 0.0, square, 1.0)
    factor = COULOMB / (math.pi * width_x * width_y * depth)
    green = (
        factor * jnp.exp(-((math.pi / EWALD_BETA) ** 2) * square) / (bounded * damping * damping)
    )
    return jnp.where(square > 0.0, green, 0.0)


def tables(length):
    indices = jnp.arange(length)
    angles = jnp.mod(indices[:, None] * indices[None, :], length).astype(jnp.float32) * (
        2.0 * math.pi / length
    )
    return (jnp.cos(angles), jnp.sin(angles))


def depth_table(modes, length):
    wave_ids = jnp.arange(modes)
    cell_ids = jnp.arange(length)
    angles = jnp.mod(wave_ids[:, None] * cell_ids[None, :], length).astype(jnp.float32) * (
        2.0 * math.pi / length
    )
    return jnp.stack([jnp.cos(angles), -jnp.sin(angles)])


def complex_table(cosine, sine, sign):
    upper = jnp.stack([cosine, sign * sine], axis=1)
    lower = jnp.stack([-sign * sine, cosine], axis=1)
    return jnp.stack([upper, lower])


def per_device(atom_x, atom_y, atom_z, charges, counts, background):
    slots = atom_x.shape[-1]
    cells_y, cells_x, depth = background.shape
    parts_x = lax.axis_size("gx")
    parts_y = lax.axis_size(("gy", "gz"))
    width_x = cells_x * parts_x
    width_y = cells_y * parts_y
    live = jnp.arange(slots) < counts.reshape(())
    charge_live = jnp.where(live, charges.reshape(slots), 0.0)
    stencil = weights(
        atom_x.reshape(slots), atom_y.reshape(slots), atom_z.reshape(slots), cells_x, cells_y, depth
    )
    spread = deposit(stencil, charge_live)
    wide = extended(spread, (("gx", 1), (("gy", "gz"), 0)), 2)
    rows_done = (
        wide[4 : cells_y + 4].at[:2].add(wide[:2]).at[cells_y - 2 :].add(wide[cells_y + 6 :])
    )
    charge_grid = (
        rows_done[:, 4 : cells_x + 4]
        .at[:, :2]
        .add(rows_done[:, :2])
        .at[:, cells_x - 2 :]
        .add(rows_done[:, cells_x + 6 :])
    )
    charge_grid = charge_grid + background
    plane_count = (depth // 2 + 1 + parts_x - 1) // parts_x * parts_x
    wave_table = depth_table(plane_count, depth)
    cos_x, sin_x = tables(width_x)
    cos_y, sin_y = tables(width_y)
    ahead_x = complex_table(cos_x, sin_x, -1.0)
    ahead_y = complex_table(cos_y, sin_y, -1.0)
    back_x = complex_table(cos_x, sin_x, 1.0)
    back_y = complex_table(cos_y, sin_y, 1.0)
    spectrum = jnp.einsum("dkz,yxz->dkyx", wave_table, charge_grid, precision=PRECISE)

    def along_x(block):
        return jnp.einsum("ckyx,cxdm->dmky", block, ahead_x, precision=PRECISE)

    columns = along_x(lax.all_to_all(spectrum, "gx", split_axis=1, concat_axis=3, tiled=True))
    lines = jnp.einsum(
        "cxky,cydn->dnxk",
        lax.all_to_all(columns, ("gy", "gz"), split_axis=1, concat_axis=3, tiled=True),
        ahead_y,
        precision=PRECISE,
    )
    strip = lines.shape[2]
    planes = lines.shape[3]
    wave_z = lax.axis_index("gx") * planes + jnp.arange(planes)
    wave_x = lax.axis_index(("gy", "gz")) * strip + jnp.arange(strip)
    green = influence(wave_z, wave_x, jnp.arange(width_y), depth, width_x, width_y)
    edge_plane = (wave_z == 0) | (2 * wave_z == depth)
    plane_weight = jnp.where(edge_plane, 1.0, 2.0)
    plane_weight = jnp.where(2 * wave_z <= depth, plane_weight, 0.0)
    green = green * plane_weight[:, None, None]
    solved = lines * jnp.transpose(green, (2, 1, 0))[None]
    inverse = jnp.einsum("cnxk,cndy->dyxk", solved, back_y, precision=PRECISE)
    result = jnp.einsum(
        "cymk,cmdx->dxyk",
        lax.all_to_all(inverse, ("gy", "gz"), split_axis=1, concat_axis=2, tiled=True),
        back_x,
        precision=PRECISE,
    )
    potential = jnp.einsum(
        "dxyk,dkz->yxz",
        lax.all_to_all(result, "gx", split_axis=1, concat_axis=3, tiled=True),
        wave_table,
        precision=PRECISE,
    )
    potential = extended(potential, (("gx", 1), (("gy", "gz"), 0)), 2)
    forces = pull(potential, stencil, charge_live)
    return forces.reshape(3, 1, 1, slots)


def solution(mesh):
    in_specs = (
        P("gx", ("gy", "gz"), None),
        P("gx", ("gy", "gz"), None),
        P("gx", ("gy", "gz"), None),
        P("gx", ("gy", "gz"), None),
        P("gx", ("gy", "gz")),
        P(("gy", "gz"), "gx", None),
    )
    out_specs = P(None, "gx", ("gy", "gz"), None)
    return jax.shard_map(
        per_device, mesh=mesh, in_specs=in_specs, out_specs=out_specs, check_vma=False
    )
```

profile of v0, /device:TPU:0, one launch (start us, length us, event | category | flops | bytes accessed | tf_op | source)
XLA Modules:
  0.0 1233.9 jit_solution(1380806359779844134)
XLA Ops:
  40.9 17.3 %fusion.6 = f32[2,196,48,96]{1,3,2,0:T(8,128)} fusion(f32[48,96,384]{2,1,0:T(8,128)S(1)} %fusion.114, f32[48,96,384]{2,1,0:T(8,128)S(1)} %bitcast.132, f32[1,196,384]{2,1,0:T(8,128)S(1)} %get-tuple-element.77, f32[1,196,384]{2,1,0:T(8,128)S(1)} %get-tuple-element.78), kind=kOutput, calls=%fused_computation.12 | convolution fusion | flops 8325516288 | bytes 21983232 | tf_op jit(solution)/shard_map/dkz,yxz->dkyx/dot_general | solution.py:165
  81.4 205.0 %all-to-all-done = f32[2,196,48,96]{3,2,0,1:T(8,128)} async-done(((f32[2,196,48,96]{3,2,0,1:T(8,128)}), f32[2,196,48,96]{3,2,0,1:T(8,128)}, u32[]{:S(2)}, u32[]{:S(2)}) %all-to-all-start) | async-done | bytes 7225376 | tf_op jit(solution)/shard_map/all_to_all | solution.py:170
  311.6 24.0 %convolution_bitcast_fusion.1 = f32[2,384,49,48]{1,2,3,0:T(8,128)} fusion(f32[2,49,48,384,1]{3,1,0,2,4:T(8,128)} %reshape.633, f32[1,384,2,384]{3,1,0,2:T(8,128)S(1)} %get-tuple-element.67, f32[1,384,2,384]{3,1,0,2:T(8,128)} %get-tuple-element.70), kind=kOutput, calls=%fused_computation.32 | convolution fusion | flops 16647782400 | bytes 16809984 | tf_op jit(solution)/shard_map/ckyx,cxdm->dmky/dot_general | solution.py:168
  335.7 18.1 %copy.32 = f32[2,384,49,48]{2,3,0,1:T(8,128)} copy(f32[2,384,49,48]{1,2,3,0:T(8,128)} %convolution_bitcast_fusion.1) | data formatting | bytes 14450688 | tf_op jit(solution)/shard_map/ckyx,cxdm->dmky/dot_general | solution.py:168
  353.8 25.9 %reshape.651 = f32[8,1,225792]{2,1,0:T(1,128)} reshape(f32[384,2,48,49]{3,2,1,0:T(8,128)} %bitcast.123) | data formatting | bytes 14450688
  388.6 77.6 %all-to-all-done.1 = f32[8,1,225792]{2,1,0:T(1,128)} async-done(((f32[8,1,225792]{2,1,0:T(1,128)}), f32[8,1,225792]{2,1,0:T(1,128)}, u32[]{:S(2)}, u32[]{:S(2)}) %all-to-all-start.1) | async-done | bytes 7225376 | tf_op jit(solution)/shard_map/all_to_all | solution.py:173
  466.7 22.7 %reduce.8 = f32[8,225792]{1,0:T(8,128)} reduce(f32[8,1,225792]{2,1,0:T(1,128)} %all-to-all-done.1, f32[]{:T(128)} %broadcast.960), dimensions={1}, to_apply=%all_to_all.56.reduce_sub_computation | reduce | bytes 14450692 | tf_op jit(solution)/shard_map/all_to_all | solution.py:173
  489.4 36.5 %reshape.652 = f32[384,2,48,49]{3,2,1,0:T(8,128)} reshape(f32[8,225792]{1,0:T(8,128)} %reduce.8) | data formatting | bytes 14450688
  525.9 21.2 %copy.64 = f32[2,48,49,8,48]{4,3,2,0,1:T(8,128)} copy(f32[2,48,49,8,48]{2,4,0,1,3:T(8,128)} %bitcast.124) | data formatting | bytes 14450688 | tf_op jit(solution)/shard_map/all_to_all | solution.py:173
  563.3 25.2 %fusion.4 = f32[2,384,48,49,1]{1,3,4,0,2:T(8,128)S(1)} fusion(f32[2,48,49,384,1]{3,2,0,1,4:T(8,128)} %reshape.635, f32[1,384,2,384]{3,1,0,2:T(8,128)S(1)} %get-tuple-element.67, f32[1,384,2,384]{3,1,0,2:T(8,128)} %get-tuple-element.70), kind=kOutput, calls=%fused_computation.7 | convolution fusion | flops 16647782400 | bytes 16809984 | tf_op jit(solution)/shard_map/cxky,cydn->dnxk/dot_general | solution.py:171
  588.5 23.0 %fusion.20 = f32[2,384,48,49]{1,3,2,0:T(8,128)} fusion(f32[2,384,48,49,1]{1,3,4,0,2:T(8,128)S(1)} %fusion.4, f32[384,48,49]{0,2,1:T(8,128)S(1)} %copy-done, f32[1,384,2,384]{3,1,2,0:T(8,128)S(1)} %get-tuple-element.71, f32[1,384,2,384]{3,1,2,0:T(8,128)S(1)} %get-tuple-element.66), kind=kOutput, calls=%fused_computation.30 | convolution fusion | flops 16649588736 | bytes 20422656 | tf_op jit(solution)/shard_map/cnxk,cndy->dyxk/dot_general | solution.py:187
  611.4 18.1 %copy.37 = f32[2,384,48,49]{3,2,0,1:T(8,128)} copy(f32[2,384,48,49]{1,3,2,0:T(8,128)} %fusion.20) | data formatting | bytes 14450688 | tf_op jit(solution)/shard_map/cnxk,cndy->dyxk/dot_general | solution.py:187
  629.6 25.9 %reshape.653 = f32[8,1,225792]{2,1,0:T(1,128)} reshape(f32[384,2,48,49]{3,2,1,0:T(8,128)} %bitcast.125) | data formatting | bytes 14450688
  655.5 87.1 %all_to_all.72 = f32[8,1,225792]{2,1,0:T(1,128)} all-to-all(f32[8,1,225792]{2,1,0:T(1,128)} %reshape.653), channel_id=1, replica_groups=mesh['gx'=4,'gy'=2,'gz'=4] {'gy','gz'}, dimensions={0} | all-to-all | bytes 14450688 | tf_op jit(solution)/shard_map/all_to_all | solution.py:190
  742.6 22.4 %reduce.9 = f32[8,225792]{1,0:T(8,128)} reduce(f32[8,1,225792]{2,1,0:T(1,128)} %all_to_all.72, f32[]{:T(128)} %broadcast.960), dimensions={1}, to_apply=%all_to_all.60.reduce_sub_computation | reduce | bytes 14450692 | tf_op jit(solution)/shard_map/all_to_all | solution.py:190
  765.0 36.6 %reshape.654 = f32[384,2,48,49]{3,2,1,0:T(8,128)} reshape(f32[8,225792]{1,0:T(8,128)} %reduce.9) | data formatting | bytes 14450688
  801.6 21.2 %copy.67 = f32[2,48,8,48,49]{3,2,4,0,1:T(8,128)} copy(f32[2,48,8,48,49]{4,3,0,1,2:T(8,128)} %bitcast.126) | data formatting | bytes 14450688 | tf_op jit(solution)/shard_map/all_to_all | solution.py:190
  839.0 23.6 %convolution_bitcast_fusion = f32[2,384,48,49]{1,3,2,0:T(8,128)} fusion(f32[2,48,384,49,1]{2,3,0,1,4:T(8,128)} %reshape.641, f32[1,384,2,384]{3,1,2,0:T(8,128)S(1)} %get-tuple-element.71, f32[1,384,2,384]{3,1,2,0:T(8,128)S(1)} %get-tuple-element.66), kind=kOutput, calls=%fused_computation.31 | convolution fusion | flops 16647782400 | bytes 16809984 | tf_op jit(solution)/shard_map/cymk,cmdx->dxyk/dot_general | solution.py:188
  862.5 18.1 %copy.42 = f32[2,384,48,49]{3,2,0,1:T(8,128)} copy(f32[2,384,48,49]{1,3,2,0:T(8,128)} %convolution_bitcast_fusion) | data formatting | bytes 14450688 | tf_op jit(solution)/shard_map/cymk,cmdx->dxyk/dot_general | solution.py:188
  880.7 39.1 %reshape.655 = f32[4,1,451584]{2,1,0:T(1,128)} reshape(f32[384,2,48,49]{3,2,1,0:T(8,128)} %bitcast.127) | data formatting | bytes 14450688
  919.8 165.2 %all_to_all.73 = f32[4,1,451584]{2,1,0:T(1,128)} all-to-all(f32[4,1,451584]{2,1,0:T(1,128)} %reshape.655), channel_id=1, replica_groups=mesh['gx'=4,'gy'=2,'gz'=4] {'gx'}, dimensions={0} | all-to-all | bytes 14450688 | tf_op jit(solution)/shard_map/all_to_all | solution.py:196
  1085.1 24.1 %reduce.10 = f32[4,451584]{1,0:T(4,128)} reduce(f32[4,1,451584]{2,1,0:T(1,128)} %all_to_all.73, f32[]{:T(128)} %broadcast.960), dimensions={1}, to_apply=%all_to_all.64.reduce_sub_computation | reduce | bytes 14450692 | tf_op jit(solution)/shard_map/all_to_all | solution.py:196
  1109.1 37.4 %reshape.656 = f32[384,2,48,49]{3,2,1,0:T(8,128)} reshape(f32[4,451584]{1,0:T(4,128)} %reduce.10) | data formatting | bytes 14450688
  1167.9 21.7 %fusion.23 = f32[48,96,384]{2,1,0:T(8,128)S(1)} fusion(f32[2,96,48,196]{1,2,3,0:T(8,128)S(1)} %bitcast.129, f32[1,196,384]{2,1,0:T(8,128)S(1)} %copy-done.2, f32[1,196,384]{2,1,0:T(8,128)S(1)} %copy-done.4), kind=kOutput, calls=%fused_computation.33 | convolution fusion | flops 8323746816 | bytes 14905344 | tf_op jit(solution)/shard_map/dxyk,dkz->yxz/dot_general | solution.py:194
  (96 shorter events, 195.5 us)
Async XLA Ops:
  0.0 27.7 %copy-start.8 = (f32[384]{0:T(512)}, f32[384]{0:T(512)S(1)}, u32[]{:S(2)}) copy-start(f32[384]{0:T(512)S(1)} %iota_convert_fusion) | copy-start | bytes 4612
  2.2 25.5 %copy-start.5 = (f32[100,256]{1,0:T(8,128)}, f32[100,256]{1,0:T(8,128)S(1)}, u32[]{:S(2)}) copy-start(f32[100,256]{1,0:T(8,128)S(1)} %get-tuple-element.73) | copy-start | bytes 307204
  14.0 9.6 collective-permute-start.1
  19.1 7.7 collective-permute-start
  20.4 18.8 %copy-start.1 = (f32[1,196,384]{2,1,0:T(8,128)}, f32[1,196,384]{2,1,0:T(8,128)S(1)}, u32[]{:S(2)}) copy-start(f32[1,196,384]{2,1,0:T(8,128)S(1)} %get-tuple-element.77) | copy-start | bytes 903172
  20.4 18.8 %copy-start.3 = (f32[1,196,384]{2,1,0:T(8,128)}, f32[1,196,384]{2,1,0:T(8,128)S(1)}, u32[]{:S(2)}) copy-start(f32[1,196,384]{2,1,0:T(8,128)S(1)} %get-tuple-element.78) | copy-start | bytes 903172
  27.7 9.0 collective-permute-start.2
  27.7 10.1 collective-permute-start.3
  69.1 217.2 %all-to-all-start = ((f32[2,196,48,96]{3,2,0,1:T(8,128)}), f32[2,196,48,96]{3,2,0,1:T(8,128)}, u32[]{:S(2)}, u32[]{:S(2)}) async-start(f32[2,196,48,96]{3,2,0,1:T(8,128)} %copy.28), calls=%async_computation | async-start | bytes 19267584 | tf_op jit(solution)/shard_map/all_to_all | solution.py:170
  379.7 86.4 %all-to-all-start.1 = ((f32[8,1,225792]{2,1,0:T(1,128)}), f32[8,1,225792]{2,1,0:T(1,128)}, u32[]{:S(2)}, u32[]{:S(2)}) async-start(f32[8,1,225792]{2,1,0:T(1,128)} %reshape.651), calls=%async_computation.1 | async-start | bytes 14450688 | tf_op jit(solution)/shard_map/all_to_all | solution.py:173
  563.3 25.2 %copy-start = (f32[384,48,49]{0,2,1:T(8,128)S(1)}, f32[384,48,49]{0,2,1:T(8,128)}, u32[]{:S(2)}) copy-start(f32[384,48,49]{0,2,1:T(8,128)} %fusion.13) | copy-start | bytes 10838020
  1163.3 4.6 copy-start.2
  1163.3 4.6 copy-start.4
  1189.6 18.0 %copy-start.6 = (f32[100,256]{1,0:T(8,128)S(1)}, f32[100,256]{1,0:T(8,128)}, u32[]{:S(2)}) copy-start(f32[100,256]{1,0:T(8,128)} %copy-done.5) | copy-start | bytes 307204
  1189.6 18.0 %copy-start.9 = (f32[384]{0:T(512)S(1)}, f32[384]{0:T(512)}, u32[]{:S(2)}) copy-start(f32[384]{0:T(512)} %copy-done.8) | copy-start | bytes 4612
  1189.6 18.0 %copy-start.14 = (f32[1,1,256]{2,1,0:T(1,128)S(1)}, f32[1,1,256]{2,1,0:T(1,128)}, u32[]{:S(2)}) copy-start(f32[1,1,256]{2,1,0:T(1,128)} %param.16) | copy-start | bytes 3076
  1189.7 6.2 collective-permute-start.5
  1191.8 6.9 collective-permute-start.4
  1198.8 7.9 collective-permute-start.7
  1198.8 21.0 %copy-start.7 = (f32[100,256]{1,0:T(8,128)S(1)}, f32[100,256]{1,0:T(8,128)}, u32[]{:S(2)}) copy-start(f32[100,256]{1,0:T(8,128)} %get-tuple-element.72) | copy-start | bytes 307204
  1198.8 8.7 collective-permute-start.6
  1219.8 13.1 %copy-start.10 = (f32[1,1,256]{2,1,0:T(1,128)S(1)}, f32[1,1,256]{2,1,0:T(1,128)}, u32[]{:S(2)}) copy-start(f32[1,1,256]{2,1,0:T(1,128)} %param.15) | copy-start | bytes 3076
  1219.8 13.1 %copy-start.13 = (f32[52]{0:T(128)S(1)}, f32[52]{0:T(128)}, u32[]{:S(2)}) copy-start(f32[52]{0:T(128)} %copy-done.12) | copy-start | bytes 628
  1219.8 13.2 %copy-start.11 = (f32[1,1,256]{2,1,0:T(1,128)S(1)}, f32[1,1,256]{2,1,0:T(1,128)}, u32[]{:S(2)}) copy-start(f32[1,1,256]{2,1,0:T(1,128)} %param.17) | copy-start | bytes 3076
  (3 other events, 8.9 us)
where the time goes:
time: 1250 us; the launch traced here: 1230 us
  local copies, waits for them, and re-layouts  393 us (31%)
  waiting for transfers between devices  309 us (25%)
  blocking collectives  252 us (20%)
  matrix products  170 us (14%)
  other arithmetic  86.9 us (7%)
  starting transfers between devices  21.7 us (2%)
    all_to_all x1, waiting for transfers between devices, per_device(): lax.all_to_all(spectrum, 'gx', split_axis=1, concat_axis=3, tiled=True)  205 us
    unnamed x40, local copies, waits for them, and re-layouts  203 us
    all_to_all x1, blocking collectives, per_device(): lax.all_to_all(result, 'gx', split_axis=1, concat_axis=3, tiled=True)  165 us
    all_to_all x1, blocking collectives, per_device(): lax.all_to_all(inverse, ('gy', 'gz'), split_axis=1, concat_axis=2, tiled=...  87.1 us
    all_to_all x1, waiting for transfers between devices, per_device(): lax.all_to_all(columns, ('gy', 'gz'), split_axis=1, concat_axis=3, tiled=...  77.6 us
    all_to_all x3, local copies, waits for them, and re-layouts, per_device(): lax.all_to_all(columns, ('gy', 'gz'), split_axis=1, concat_axis=3, tiled=...  37.9 us
    all_to_all x2, local copies, waits for them, and re-layouts, per_device(): lax.all_to_all(inverse, ('gy', 'gz'), split_axis=1, concat_axis=2, tiled=...  37.4 us
    all_to_all x2, local copies, waits for them, and re-layouts, per_device(): lax.all_to_all(spectrum, 'gx', split_axis=1, concat_axis=3, tiled=True)  25.3 us
  transfers between devices with their start and end apart: 10, of which 9 were waited for; matrix products, arithmetic and copies ran while one was open for 1% of the time, Pallas kernels for 0%

commit v1 on v0

--- a/solution.py
+++ b/solution.py
@@ -7,6 +7,13 @@
 COULOMB = 6.5
 EWALD_BETA = 1.0
 PRECISE = lax.Precision.HIGHEST
+
+
+def swap_blocks(x, axis, split, join):
+    peers = lax.axis_size(axis)
+    pieces = jnp.stack(jnp.split(x, peers, axis=split), axis=0)
+    pieces = lax.all_to_all(pieces, axis, split_axis=0, concat_axis=0)
+    return jnp.concatenate(pieces, axis=join)
 
 
 def extended(block, sides, width):
@@ -192,10 +199,7 @@
         precision=PRECISE,
     )
     potential = jnp.einsum(
-        "dxyk,dkz->yxz",
-        lax.all_to_all(result, "gx", split_axis=1, concat_axis=3, tiled=True),
-        wave_table,
-        precision=PRECISE,
+        "dxyk,dkz->yxz", swap_blocks(result, "gx", 1, 3), wave_table, precision=PRECISE
     )
     potential = extended(potential, (("gx", 1), (("gy", "gz"), 0)), 2)
     forces = pull(potential, stencil, charge_live)

time: 1250 us -> 1180 us (0.944)
  local copies, waits for them, and re-layouts: 393 us -> 298 us
  blocking collectives: 252 us -> 305 us
  other arithmetic: 86.9 us -> 67.1 us
    unnamed x40 -> x38, local copies, waits for them, and re-layouts: 203 us -> 127 us
    all_to_all x1, blocking collectives: 165 us -> 218 us  [swap_blocks(): pieces = lax.all_to_all(pieces, axis, split_axis=0, concat_axis=0)]
    all_to_all x1 -> x0, other arithmetic: 24.1 us -> none  [per_device(): lax.all_to_all(result, 'gx', split_axis=1, concat_axis=3, tiled=True)]
    all_to_all x2 -> x0, local copies, waits for them, and re-layouts: 21.3 us -> none  [per_device(): lax.all_to_all(result, 'gx', split_axis=1, concat_axis=3, tiled=True)]
    dot_general x1 -> x0, local copies, waits for them, and re-layouts: 18.1 us -> none  [per_device(): jnp.einsum('cymk,cmdx->dxyk', lax.all_to_all(inverse, ('gy', 'gz'), split...]
    another operation x0 -> x2, local copies, waits for them, and re-layouts: none -> 16.7 us  [swap_blocks(): pieces = jnp.stack(jnp.split(x, peers, axis=split), axis=0)]
where the time goes in v1:
time: 1180 us; the launch traced here: 1170 us
  waiting for transfers between devices  309 us (26%)
  blocking collectives  305 us (26%)
  local copies, waits for them, and re-layouts  298 us (25%)
  matrix products  171 us (14%)
  other arithmetic  67.1 us (6%)
  starting transfers between devices  21.8 us (2%)
    all_to_all x1, blocking collectives, swap_blocks(): pieces = lax.all_to_all(pieces, axis, split_axis=0, concat_axis=0)  218 us
    all_to_all x1, waiting for transfers between devices, per_device(): lax.all_to_all(spectrum, 'gx', split_axis=1, concat_axis=3, tiled=True)  205 us
    unnamed x38, local copies, waits for them, and re-layouts  127 us
    all_to_all x1, blocking collectives, per_device(): lax.all_to_all(inverse, ('gy', 'gz'), split_axis=1, concat_axis=2, tiled=...  87.1 us
    all_to_all x1, waiting for transfers between devices, per_device(): lax.all_to_all(columns, ('gy', 'gz'), split_axis=1, concat_axis=3, tiled=...  77.5 us
    all_to_all x3, local copies, waits for them, and re-layouts, per_device(): lax.all_to_all(columns, ('gy', 'gz'), split_axis=1, concat_axis=3, tiled=...  37.9 us
    all_to_all x2, local copies, waits for them, and re-layouts, per_device(): lax.all_to_all(inverse, ('gy', 'gz'), split_axis=1, concat_axis=2, tiled=...  37.3 us
    all_to_all x2, local copies, waits for them, and re-layouts, per_device(): lax.all_to_all(spectrum, 'gx', split_axis=1, concat_axis=3, tiled=True)  25.3 us
  transfers between devices with their start and end apart: 10, of which 9 were waited for; matrix products, arithmetic and copies ran while one was open for 1% of the time, Pallas kernels for 0%

profile of v1, /device:TPU:0, one launch (start us, length us, event | category | flops | bytes accessed | tf_op | source)
XLA Modules:
  0.0 1172.4 jit_solution(16861791548499330366)
XLA Ops:
  40.9 17.4 %fusion.6 = f32[2,196,48,96]{1,3,2,0:T(8,128)} fusion(f32[48,96,384]{2,1,0:T(8,128)S(1)} %fusion.114, f32[48,96,384]{2,1,0:T(8,128)S(1)} %bitcast.135, f32[1,196,384]{2,1,0:T(8,128)S(1)} %get-tuple-element.81, f32[1,196,384]{2,1,0:T(8,128)S(1)} %get-tuple-element.82), kind=kOutput, calls=%fused_computation.13 | convolution fusion | flops 8325516288 | bytes 21983232 | tf_op jit(solution)/shard_map/dkz,yxz->dkyx/dot_general | solution.py:172
  81.5 205.0 %all-to-all-done = f32[2,196,48,96]{3,2,0,1:T(8,128)} async-done(((f32[2,196,48,96]{3,2,0,1:T(8,128)}), f32[2,196,48,96]{3,2,0,1:T(8,128)}, u32[]{:S(2)}, u32[]{:S(2)}) %all-to-all-start) | async-done | bytes 7225376 | tf_op jit(solution)/shard_map/all_to_all | solution.py:177
  286.5 13.6 %copy.58 = f32[2,49,48,4,96]{4,3,1,0,2:T(4,128)} copy(f32[2,49,48,4,96]{4,2,0,1,3:T(8,128)} %bitcast.21) | data formatting | bytes 14450688 | tf_op jit(solution)/shard_map/all_to_all | solution.py:177
  311.8 24.1 %convolution_bitcast_fusion.1 = f32[2,384,49,48]{1,2,3,0:T(8,128)} fusion(f32[2,49,48,384,1]{3,1,0,2,4:T(8,128)} %reshape.641, f32[1,384,2,384]{3,1,0,2:T(8,128)S(1)} %get-tuple-element.71, f32[1,384,2,384]{3,1,0,2:T(8,128)} %get-tuple-element.74), kind=kOutput, calls=%fused_computation.33 | convolution fusion | flops 16647782400 | bytes 16809984 | tf_op jit(solution)/shard_map/ckyx,cxdm->dmky/dot_general | solution.py:175
  335.9 18.1 %copy.30 = f32[2,384,49,48]{2,3,0,1:T(8,128)} copy(f32[2,384,49,48]{1,2,3,0:T(8,128)} %convolution_bitcast_fusion.1) | data formatting | bytes 14450688 | tf_op jit(solution)/shard_map/ckyx,cxdm->dmky/dot_general | solution.py:175
  354.0 25.9 %reshape.659 = f32[8,1,225792]{2,1,0:T(1,128)} reshape(f32[384,2,48,49]{3,2,1,0:T(8,128)} %bitcast.128) | data formatting | bytes 14450688
  388.8 77.5 %all-to-all-done.1 = f32[8,1,225792]{2,1,0:T(1,128)} async-done(((f32[8,1,225792]{2,1,0:T(1,128)}), f32[8,1,225792]{2,1,0:T(1,128)}, u32[]{:S(2)}, u32[]{:S(2)}) %all-to-all-start.1) | async-done | bytes 7225376 | tf_op jit(solution)/shard_map/all_to_all | solution.py:180
  466.9 22.6 %reduce.8 = f32[8,225792]{1,0:T(8,128)} reduce(f32[8,1,225792]{2,1,0:T(1,128)} %all-to-all-done.1, f32[]{:T(128)} %broadcast.960), dimensions={1}, to_apply=%all_to_all.46.reduce_sub_computation | reduce | bytes 14450692 | tf_op jit(solution)/shard_map/all_to_all | solution.py:180
  489.6 36.5 %reshape.660 = f32[384,2,48,49]{3,2,1,0:T(8,128)} reshape(f32[8,225792]{1,0:T(8,128)} %reduce.8) | data formatting | bytes 14450688
  526.1 21.1 %copy.61 = f32[2,48,49,8,48]{4,3,2,0,1:T(8,128)} copy(f32[2,48,49,8,48]{2,4,0,1,3:T(8,128)} %bitcast.129) | data formatting | bytes 14450688 | tf_op jit(solution)/shard_map/all_to_all | solution.py:180
  547.3 16.2 %reshape.643 = f32[2,48,49,384,1]{3,2,0,1,4:T(8,128)} reshape(f32[2,48,49,8,48]{4,3,2,0,1:T(8,128)} %copy.61) | data formatting | bytes 14450688 | tf_op jit(solution)/shard_map/all_to_all | solution.py:180
  563.5 25.2 %fusion.4 = f32[2,384,48,49,1]{1,3,4,0,2:T(8,128)S(1)} fusion(f32[2,48,49,384,1]{3,2,0,1,4:T(8,128)} %reshape.643, f32[1,384,2,384]{3,1,0,2:T(8,128)S(1)} %get-tuple-element.71, f32[1,384,2,384]{3,1,0,2:T(8,128)} %get-tuple-element.74), kind=kOutput, calls=%fused_computation.8 | convolution fusion | flops 16647782400 | bytes 16809984 | tf_op jit(solution)/shard_map/cxky,cydn->dnxk/dot_general | solution.py:178
  588.6 23.0 %fusion.20 = f32[2,384,48,49]{1,3,2,0:T(8,128)} fusion(f32[2,384,48,49,1]{1,3,4,0,2:T(8,128)S(1)} %fusion.4, f32[384,48,49]{0,2,1:T(8,128)S(1)} %copy-done, f32[1,384,2,384]{3,1,2,0:T(8,128)S(1)} %get-tuple-element.75, f32[1,384,2,384]{3,1,2,0:T(8,128)S(1)} %get-tuple-element.70), kind=kOutput, calls=%fused_computation.31 | convolution fusion | flops 16649588736 | bytes 20422656 | tf_op jit(solution)/shard_map/cnxk,cndy->dyxk/dot_general | solution.py:194
  611.7 18.1 %copy.35 = f32[2,384,48,49]{3,2,0,1:T(8,128)} copy(f32[2,384,48,49]{1,3,2,0:T(8,128)} %fusion.20) | data formatting | bytes 14450688 | tf_op jit(solution)/shard_map/cnxk,cndy->dyxk/dot_general | solution.py:194
  629.8 25.9 %reshape.661 = f32[8,1,225792]{2,1,0:T(1,128)} reshape(f32[384,2,48,49]{3,2,1,0:T(8,128)} %bitcast.130) | data formatting | bytes 14450688
  655.7 87.1 %all_to_all.59 = f32[8,1,225792]{2,1,0:T(1,128)} all-to-all(f32[8,1,225792]{2,1,0:T(1,128)} %reshape.661), channel_id=1, replica_groups=mesh['gx'=4,'gy'=2,'gz'=4] {'gy','gz'}, dimensions={0} | all-to-all | bytes 14450688 | tf_op jit(solution)/shard_map/all_to_all | solution.py:197
  742.8 22.4 %reduce.9 = f32[8,225792]{1,0:T(8,128)} reduce(f32[8,1,225792]{2,1,0:T(1,128)} %all_to_all.59, f32[]{:T(128)} %broadcast.960), dimensions={1}, to_apply=%all_to_all.50.reduce_sub_computation | reduce | bytes 14450692 | tf_op jit(solution)/shard_map/all_to_all | solution.py:197
  765.2 36.8 %reshape.662 = f32[384,2,48,49]{3,2,1,0:T(8,128)} reshape(f32[8,225792]{1,0:T(8,128)} %reduce.9) | data formatting | bytes 14450688
  802.0 21.1 %copy.64 = f32[2,48,8,48,49]{3,2,4,0,1:T(8,128)} copy(f32[2,48,8,48,49]{4,3,0,1,2:T(8,128)} %bitcast.131) | data formatting | bytes 14450688 | tf_op jit(solution)/shard_map/all_to_all | solution.py:197
  823.1 16.2 %reshape.649 = f32[2,48,384,49,1]{2,3,0,1,4:T(8,128)} reshape(f32[2,48,8,48,49]{3,2,4,0,1:T(8,128)} %copy.64) | data formatting | bytes 14450688 | tf_op jit(solution)/shard_map/all_to_all | solution.py:197
  839.3 23.6 %convolution_bitcast_fusion = f32[2,384,48,49]{1,3,2,0:T(8,128)} fusion(f32[2,48,384,49,1]{2,3,0,1,4:T(8,128)} %reshape.649, f32[1,384,2,384]{3,1,2,0:T(8,128)S(1)} %get-tuple-element.75, f32[1,384,2,384]{3,1,2,0:T(8,128)S(1)} %get-tuple-element.70), kind=kOutput, calls=%fused_computation.32 | convolution fusion | flops 16647782400 | bytes 16809984 | tf_op jit(solution)/shard_map/cymk,cmdx->dxyk/dot_general | solution.py:195
  883.8 217.7 %all_to_all.60 = f32[4,2,96,48,49]{2,3,4,1,0:T(8,128)} all-to-all(f32[4,2,96,48,49]{2,3,4,1,0:T(8,128)} %copy.40), channel_id=1, replica_groups=mesh['gx'=4,'gy'=2,'gz'=4] {'gx'}, dimensions={0} | all-to-all | bytes 14450688 | tf_op jit(solution)/shard_map/all_to_all | solution.py:15
  1106.1 21.7 %fusion.23 = f32[48,96,384]{2,1,0:T(8,128)S(1)} fusion(f32[2,96,48,196]{1,2,3,0:T(8,128)S(1)} %bitcast.132, f32[1,196,384]{2,1,0:T(8,128)S(1)} %copy-done.2, f32[1,196,384]{2,1,0:T(8,128)S(1)} %copy-done.4), kind=kOutput, calls=%fused_computation.34 | convolution fusion | flops 8323746816 | bytes 14905344 | tf_op jit(solution)/shard_map/dxyk,dkz->yxz/dot_general | solution.py:201
  1158.0 13.1 %multiply_reduce_fusion.2 = (f32[52,256]{1,0:T(8,128)S(1)}, f32[52,256]{1,0:T(8,128)S(1)}) fusion(f32[100,256]{1,0:T(8,128)S(1)} %copy-done.7, f32[100,256]{1,0:T(8,128)S(1)} %copy-done.6, f32[384]{0:T(512)S(1)} %copy-done.9, f32[256]{0:T(256)S(1)} %bitcast.145, f32[2,100,384]{2,1,0:T(8,128)S(1)} %collective-permute-done.7, ...), kind=kOutput, calls=%fused_computation.19 | convolution fusion | flops 6150404096 | bytes 8301056 | tf_op jit(solution)/shard_map/dot_general | solution.py:71
  (94 shorter events, 140.7 us)
Async XLA Ops:
  0.0 27.7 %copy-start.8 = (f32[384]{0:T(512)}, f32[384]{0:T(512)S(1)}, u32[]{:S(2)}) copy-start(f32[384]{0:T(512)S(1)} %iota_convert_fusion) | copy-start | bytes 4612
  2.2 25.6 %copy-start.5 = (f32[100,256]{1,0:T(8,128)}, f32[100,256]{1,0:T(8,128)S(1)}, u32[]{:S(2)}) copy-start(f32[100,256]{1,0:T(8,128)S(1)} %get-tuple-element.77) | copy-start | bytes 307204
  14.0 9.6 collective-permute-start.1
  19.1 7.7 collective-permute-start
  20.4 18.8 %copy-start.1 = (f32[1,196,384]{2,1,0:T(8,128)}, f32[1,196,384]{2,1,0:T(8,128)S(1)}, u32[]{:S(2)}) copy-start(f32[1,196,384]{2,1,0:T(8,128)S(1)} %get-tuple-element.81) | copy-start | bytes 903172
  20.4 18.8 %copy-start.3 = (f32[1,196,384]{2,1,0:T(8,128)}, f32[1,196,384]{2,1,0:T(8,128)S(1)}, u32[]{:S(2)}) copy-start(f32[1,196,384]{2,1,0:T(8,128)S(1)} %get-tuple-element.82) | copy-start | bytes 903172
  27.7 9.0 collective-permute-start.2
  27.7 10.0 collective-permute-start.3
  69.2 217.3 %all-to-all-start = ((f32[2,196,48,96]{3,2,0,1:T(8,128)}), f32[2,196,48,96]{3,2,0,1:T(8,128)}, u32[]{:S(2)}, u32[]{:S(2)}) async-start(f32[2,196,48,96]{3,2,0,1:T(8,128)} %copy.26), calls=%async_computation | async-start | bytes 19267584 | tf_op jit(solution)/shard_map/all_to_all | solution.py:177
  379.9 86.4 %all-to-all-start.1 = ((f32[8,1,225792]{2,1,0:T(1,128)}), f32[8,1,225792]{2,1,0:T(1,128)}, u32[]{:S(2)}, u32[]{:S(2)}) async-start(f32[8,1,225792]{2,1,0:T(1,128)} %reshape.659), calls=%async_computation.1 | async-start | bytes 14450688 | tf_op jit(solution)/shard_map/all_to_all | solution.py:180
  563.5 25.2 %copy-start = (f32[384,48,49]{0,2,1:T(8,128)S(1)}, f32[384,48,49]{0,2,1:T(8,128)}, u32[]{:S(2)}) copy-start(f32[384,48,49]{0,2,1:T(8,128)} %fusion.13) | copy-start | bytes 10838020
  1101.5 4.5 copy-start.2
  1101.5 4.5 copy-start.4
  1127.8 17.9 %copy-start.6 = (f32[100,256]{1,0:T(8,128)S(1)}, f32[100,256]{1,0:T(8,128)}, u32[]{:S(2)}) copy-start(f32[100,256]{1,0:T(8,128)} %copy-done.5) | copy-start | bytes 307204
  1127.8 17.9 %copy-start.9 = (f32[384]{0:T(512)S(1)}, f32[384]{0:T(512)}, u32[]{:S(2)}) copy-start(f32[384]{0:T(512)} %copy-done.8) | copy-start | bytes 4612
  1127.8 17.9 %copy-start.14 = (f32[1,1,256]{2,1,0:T(1,128)S(1)}, f32[1,1,256]{2,1,0:T(1,128)}, u32[]{:S(2)}) copy-start(f32[1,1,256]{2,1,0:T(1,128)} %param.16) | copy-start | bytes 3076
  1128.0 6.1 collective-permute-start.5
  1130.0 6.9 collective-permute-start.4
  1137.1 7.9 collective-permute-start.7
  1137.1 20.9 %copy-start.7 = (f32[100,256]{1,0:T(8,128)S(1)}, f32[100,256]{1,0:T(8,128)}, u32[]{:S(2)}) copy-start(f32[100,256]{1,0:T(8,128)} %get-tuple-element.76) | copy-start | bytes 307204
  1137.1 8.6 collective-permute-start.6
  1158.0 13.1 %copy-start.10 = (f32[1,1,256]{2,1,0:T(1,128)S(1)}, f32[1,1,256]{2,1,0:T(1,128)}, u32[]{:S(2)}) copy-start(f32[1,1,256]{2,1,0:T(1,128)} %param.15) | copy-start | bytes 3076
  1158.0 13.1 %copy-start.13 = (f32[52]{0:T(128)S(1)}, f32[52]{0:T(128)}, u32[]{:S(2)}) copy-start(f32[52]{0:T(128)} %copy-done.12) | copy-start | bytes 628
  1158.0 13.3 %copy-start.11 = (f32[1,1,256]{2,1,0:T(1,128)S(1)}, f32[1,1,256]{2,1,0:T(1,128)}, u32[]{:S(2)}) copy-start(f32[1,1,256]{2,1,0:T(1,128)} %param.17) | copy-start | bytes 3076
  (3 other events, 8.9 us)
